TPU v7x, 512 devices: a whole 4x8x8 slice. The times are simulated.
512 devices in a mesh: rows: 32 (over y_hi, z), feat: 16 (over y_lo, x, core).
Axes of the slice: x: 4, y: 8 (y_hi: 4, y_lo: 2; y = y_hi * 2 + y_lo), z: 8, core: 2. Of those that a mesh axis runs over, the one named last changes fastest.
Arguments:
- acts: bfloat16 [32768, 8192], P('rows', 'feat'), may hold values from -6 to 6
- out_grads: bfloat16 [32768, 8192], P('rows', 'feat'), may hold values from -6 to 6
- proj_in: bfloat16 [8192, 256], P('feat'), may hold values from -0.0625 to 0.0625
- proj_out: bfloat16 [8192, 256], P('feat'), may hold values from -0.0625 to 0.0625
- assignment: int32 [32768], P('rows'), may hold values from 0 to 255
- codes: int32 [4096, 65536], P('rows', 'feat'), may hold values from -128 to 127
- zero_points: int32 [65536], P('feat'), may hold values from -64 to 63
- scales: float32 [65536], P('feat'), may hold values from 2e-06 to 2e-05
Outputs:
- scores: float32 [256, 4096], P('feat', 'rows')
All inputs are finite; a program needn't handle non-finite values.
Results may differ from a plain program's by a relative error of at most 0.005.
Values may be sent and summed in bfloat16 or wider, within the bound.
No kernel may reach another device: no remote copies, remote signals or barrier semaphores. Data moves between devices by JAX's collectives and lax.ppermute only.
A program may use at most 64 MiB of HBM per device.

v0:
```python
import jax
import jax.numpy as jnp
from jax import lax
from jax.experimental import pallas as pl
from jax.experimental.pallas import tpu as pltpu
from jax.sharding import Mesh
from jax.sharding import PartitionSpec as P


RANK = 256
QUERIES = 256
AXES = ("yh", "zl", "zh", "yl", "x", "c")
ROWS = ("yh", "zl", "zh")
FEAT = ("yl", "x", "c")
NY = 4
NZ = 8
ZH = 2
ZL = 4
NW = 8
NF = 16
NI = 16
NJ = 16
HALF = NI * NJ
LANES = 128
OWNER_ROW = 128
PACKED_ROWS = 144
LINK_GAIN = 128.0
f32 = jnp.float32
bf16 = jnp.bfloat16
f16 = jnp.float16
VMEM = pl.BlockSpec(memory_space=pltpu.VMEM)
SMEM = pl.BlockSpec(memory_space=pltpu.SMEM)
SMALL = pltpu.CompilerParams(vmem_limit_bytes=16 * 2**20)


def exchange(blocks, axes):
    return lax.all_to_all(blocks, axes, 0, 0, tiled=True)


def store_kernel(codes_ref, zero_ref, *refs):
    outs, turned = refs[:ZL], refs[ZL]
    zl, c = lax.axis_index("zl"), lax.axis_index("c")
    for i in range(codes_ref.shape[1] // RANK):
        cols = slice(i * RANK, (i + 1) * RANK)
        turned[...] = (codes_ref[:, cols] - zero_ref[:, cols]).astype(f32).T
        for k in range(ZL):
            for s in range(2):
                for h in range(ZH):
                    block = (c ^ s) * NZ + (zl ^ k) * ZH + h
                    rows = pl.ds(pl.multiple_of(block * NJ, NJ), NJ)
                    outs[k][s, h, i * NJ : (i + 1) * NJ, :] = turned[rows, :].astype(bf16)


def store_levels(codes, zero_points):
    rows = codes.shape[0]
    step = 4
    return pl.pallas_call(
        store_kernel,
        grid=(NI // step,),
        in_specs=[
            pl.BlockSpec((rows, step * RANK), lambda g: (0, g)),
            pl.BlockSpec((1, step * RANK), lambda g: (0, g)),
        ],
        out_specs=[pl.BlockSpec((2, ZH, step * NJ, rows), lambda g: (0, 0, g, 0))] * ZL,
        out_shape=[jax.ShapeDtypeStruct((2, ZH, HALF, rows), bf16)] * ZL,
        scratch_shapes=[pltpu.VMEM((RANK, rows), f32)],
        compiler_params=SMALL,
        name="store_levels",
    )(codes, zero_points.reshape(1, -1))


def pick_kernel(scales_ref, own_ref, other_ref):
    c, z = lax.axis_index("c"), lax.axis_index(("zl", "zh"))
    own_ref[...] = scales_ref[:, pl.ds(c * NZ + z, 1), :]
    other_ref[...] = scales_ref[:, pl.ds((1 - c) * NZ + z, 1), :]


def pick_scales(scales):
    return pl.pallas_call(
        pick_kernel,
        in_specs=[VMEM],
        out_specs=[VMEM] * 2,
        out_shape=[jax.ShapeDtypeStruct((NI, 1, NJ), f32)] * 2,
        compiler_params=SMALL,
        name="pick_scales",
    )(scales.reshape(NI, NF, NJ))


def project_kernel(acts_ref, grads_ref, in_ref, out_ref, keep_ref, send_ref, turned, full):
    c = lax.axis_index("c")

    @pl.when(pl.program_id(0) == 0)
    def turn():
        turned[0] = in_ref[...].T
        turned[1] = out_ref[...].T

    for side, ref in enumerate((acts_ref, grads_ref)):
        full[side] = lax.dot_general(
            turned[side], ref[...], (((1,), (1,)), ((), ())), preferred_element_type=f32
        )
    for w in range(NW):
        for ref, core in ((keep_ref, c), (send_ref, 1 - c)):
            rows = pl.ds(pl.multiple_of((core * NZ + w) * NJ, NJ), NJ)
            ref[w, :NJ, :] = full[0, rows, :]
            rows = pl.ds(pl.multiple_of((w * 2 + core) * NI, NI), NI)
            ref[w, NJ:, :] = full[1, rows, :]


def project(acts, out_grads, proj_in, proj_out):
    tokens, depth = acts.shape
    span = 2 * LANES
    wide = pl.BlockSpec((span, depth), lambda g: (g, 0))
    whole = pl.BlockSpec((depth, RANK), lambda g: (0, 0))
    shape = jax.ShapeDtypeStruct((NW, NJ + NI, tokens), f32)
    return pl.pallas_call(
        project_kernel,
        grid=(tokens // span,),
        in_specs=[wide, wide, whole, whole],
        out_specs=[pl.BlockSpec((NW, NJ + NI, span), lambda g: (0, 0, g))] * 2,
        out_shape=[shape] * 2,
        scratch_shapes=[pltpu.VMEM((2, RANK, depth), bf16), pltpu.VMEM((2, RANK, span), f32)],
        name="project",
    )(acts, out_grads, proj_in, proj_out)


def pack_kernel(sums_ref, owner_ref, inner_ref, packed_ref):
    values = sums_ref[...] * (1.0 / LINK_GAIN)
    inner_ref[...] = values[:NJ].astype(bf16)
    outer = values[NJ:].astype(bf16)
    owners = owner_ref[...].astype(f32)
    tail = jnp.concatenate([owners, jnp.zeros_like(owners)], axis=0).astype(bf16)
    for r in range(NZ):
        for t in range(NZ):
            packed_ref[r, t * NI : (t + 1) * NI, :] = outer[:, t * LANES : (t + 1) * LANES]
        packed_ref[r, OWNER_ROW:, :] = tail


def pack_tokens(sums, assignment):
    return pl.pallas_call(
        pack_kernel,
        in_specs=[VMEM] * 2,
        out_specs=[VMEM] * 2,
        out_shape=[
            jax.ShapeDtypeStruct((NJ, sums.shape[1]), bf16),
            jax.ShapeDtypeStruct((NZ, PACKED_ROWS, LANES), bf16),
        ],
        compiler_params=SMALL,
        name="pack_tokens",
    )(sums, assignment.reshape(NZ, LANES))


def grads_kernel(inner_ref, own_ref, other_ref, scale_ref, out_ref, acc):
    acc[...] = jnp.zeros_like(acc)
    tiles = 4
    span = tiles * LANES
    query = lax.broadcasted_iota(jnp.int32, (QUERIES, span), 0).astype(f32)

    def row(r, carry):
        owners = own_ref[r, OWNER_ROW:, :].astype(f32)
        for p in range(NZ // tiles):
            inner = inner_ref[r, :, p * span : (p + 1) * span].astype(f32)
            cut = range(p * tiles, (p + 1) * tiles)
            parts = []
            for ref in (own_ref, other_ref):
                outer = jnp.concatenate([ref[r, t * NI : (t + 1) * NI, :] for t in cut], axis=1).astype(f32)
                parts.append((outer[:, None, :] * inner[None, :, :]).reshape(HALF, span).astype(bf16))
            product = jnp.concatenate(parts, axis=0)
            owner = jnp.concatenate([owners[t : t + 1, :] for t in cut], axis=1)
            mine = jnp.where(query == owner, 1.0, 0.0).astype(bf16)
            acc[...] += lax.dot_general(product, mine, (((1,), (1,)), ((), ())), preferred_element_type=f32)
        return carry

    lax.fori_loop(0, NZ, row, 0, unroll=4)
    out_ref[...] = (acc[...].T * scale_ref[...]).astype(bf16)


def query_grads(inner, own, other, scale):
    return pl.pallas_call(
        grads_kernel,
        in_specs=[VMEM] * 4,
        out_specs=VMEM,
        out_shape=jax.ShapeDtypeStruct((QUERIES, 2 * HALF), bf16),
        scratch_shapes=[pltpu.VMEM((2 * HALF, QUERIES), f32)],
        compiler_params=SMALL,
        name="query_grads",
    )(inner, own, other, scale)


def share_kernel(terms_ref, out_ref):
    total = terms_ref[0].astype(f32)
    for y in range(1, NY):
        total += terms_ref[y].astype(f32)
    share = total.astype(bf16)
    for y in range(NY * ZH):
        out_ref[y] = share


def spread_share(terms):
    return pl.pallas_call(
        share_kernel,
        in_specs=[VMEM],
        out_specs=VMEM,
        out_shape=jax.ShapeDtypeStruct((NY * ZH, *terms.shape[1:]), bf16),
        compiler_params=SMALL,
        name="spread_share",
    )(terms)


def terms_kernel(late_ref, scaled_ref, other_ref, *refs):
    own, (keep_ref, send_ref) = refs[:ZL], refs[ZL:]
    zl, c = late_ref[0], lax.axis_index("c")
    for k in range(ZL):
        terms = jnp.zeros((QUERIES, other_ref.shape[3]), f32)
        for h in range(ZH):
            terms += jnp.dot(scaled_ref[h, :, :HALF], own[k][0, h], preferred_element_type=f32)
            terms += jnp.dot(scaled_ref[h, :, HALF:], other_ref[k, h], preferred_element_type=f32)
        terms = terms.reshape(NW, 2, QUERIES // NF, terms.shape[1])
        first, second = terms[:, 0], terms[:, 1]
        keep_ref[zl ^ k] = jnp.where(c == 0, first, second)
        send_ref[zl ^ k] = jnp.where(c == 0, second, first)


def score_terms(late, scaled, own, other):
    shape = jax.ShapeDtypeStruct((ZL, NW, QUERIES // NF, other.shape[3]), f32)
    return pl.pallas_call(
        terms_kernel,
        in_specs=[SMEM] + [VMEM] * (2 + ZL),
        out_specs=[VMEM] * 2,
        out_shape=[shape, shape],
        compiler_params=SMALL,
        name="score_terms",
    )(late, scaled, other, *own)


def late_kernel(place_ref, out_ref):
    for i in range(out_ref.shape[0]):
        out_ref[i] = place_ref[i]


def late_place(place):
    return pl.pallas_call(
        late_kernel,
        in_specs=[SMEM],
        out_specs=SMEM,
        out_shape=jax.ShapeDtypeStruct(place.shape, place.dtype),
        name="late_place",
    )(place)


def local(acts, out_grads, proj_in, proj_out, assignment, codes, zero_points, scales):
    flip = [(0, 1), (1, 0)]
    keep, send = project(acts, out_grads, proj_in, proj_out)
    got = lax.ppermute(send, "c", flip)
    parts = ((keep + got) * LINK_GAIN).astype(f16)
    parts = exchange(parts, ("yl", "x"))
    sums = jnp.sum(parts.astype(f32), axis=0)

    inner, packed = pack_tokens(sums, assignment)
    own = exchange(packed, ("zl", "zh"))
    swap = [(r * NW + w, w * NW + r) for r in range(NZ) for w in range(NW)]
    inner = lax.ppermute(inner, ("zl", "zh", "yl", "x"), swap)
    inner = exchange(jnp.broadcast_to(inner[None], (NW, *inner.shape)), ("yl", "x"))
    other = lax.ppermute(own, "c", flip)

    store = list(store_levels(codes, zero_points))
    for k in range(1, ZL):
        store[k] = lax.ppermute(store[k], "zl", [(r, r ^ k) for r in range(ZL)])
    store_other = lax.ppermute(jnp.stack([block[1] for block in store]), "c", flip)

    own_scale, other_scale = pick_scales(scales)
    other_scale = lax.ppermute(other_scale, "c", flip)
    scale = jnp.concatenate([own_scale, other_scale], axis=0).reshape(1, 2 * HALF)

    late = late_place(lax.axis_index("zl").reshape(1).astype(jnp.int32))
    grads = query_grads(inner, own, other, scale)
    grads = exchange(grads.reshape(NY, QUERIES // NY, 2 * HALF), "yh")
    scaled = exchange(spread_share(grads), ("zh", "yh")).reshape(ZH, QUERIES, 2 * HALF)

    keep, send = score_terms(late, scaled, store, store_other)
    got = lax.ppermute(send, "c", flip)
    terms = (keep + got).astype(bf16).reshape(ZL * NW, QUERIES // NF, codes.shape[0])
    terms = exchange(terms, ("zl", "yl", "x"))
    return jnp.sum(terms.astype(f32), axis=0)


def solution(mesh):
    split = Mesh(mesh.devices.reshape(4, 4, 2, 2, 4, 2), AXES)
    in_specs = (
        P(ROWS, FEAT),
        P(ROWS, FEAT),
        P(FEAT, None),
        P(FEAT, None),
        P(ROWS),
        P(ROWS, FEAT),
        P(FEAT),
        P(FEAT),
    )
    out_specs = P(FEAT, ROWS)
    return jax.shard_map(local, mesh=split, in_specs=in_specs, out_specs=out_specs, check_vma=False)
```

profile of v0, /device:TPU:1, one launch (start us, length us, event | category | flops | bytes accessed | tf_op | source)
XLA Modules:
  0.0 151.5 jit_solution(223308365337329535)
XLA Ops:
  0.0 5.0 %project.1 = (f32[8,32,1024]{2,1,0:T(8,128)}, f32[8,32,1024]{2,1,0:T(8,128)}) custom-call(bf16[1024,512]{1,0:T(8,128)(2,1)} %acts_ref.1, bf16[1024,512]{1,0:T(8,128)(2,1)} %grads_ref.1, bf16[512,256]{1,0:T(8,128)(2,1)} %in_ref.1, bf16[512,256]{1,0:T(8,128)(2,1)} %out_ref.1), custom_call_target="tpu_custom_call" | custom-call | tf_op jit(solution)/shard_map/project/pallas_call | solution.py:115
  5.0 8.7 %collective-permute-start = (f32[8,32,1024]{2,1,0:T(8,128)}, f32[8,32,1024]{2,1,0:T(8,128)S(1)}, u32[]{:S(2)}, u32[]{:S(2)}) collective-permute-start(f32[8,32,1024]{2,1,0:T(8,128)} %get-tuple-element.18), channel_id=1, source_target_pairs={{0,1},{1,0},{2,3},{3,2},{4,5},{5,4},{6,7},{7,6},{8,9},{9,8},{10,11... | collective-permute-start | bytes 3145736 | tf_op jit(solution)/shard_map/ppermute | solution.py:253
  13.7 2.5 %collective-permute-done = f32[8,32,1024]{2,1,0:T(8,128)S(1)} collective-permute-done((f32[8,32,1024]{2,1,0:T(8,128)}, f32[8,32,1024]{2,1,0:T(8,128)S(1)}, u32[]{:S(2)}, u32[]{:S(2)}) %collective-permute-start) | collective-permute-done | bytes 1048608 | tf_op jit(solution)/shard_map/ppermute | solution.py:253
  16.2 1.5 multiply_convert_fusion
  17.7 11.2 %all_to_all.30 = f16[8,32,1024]{2,1,0:T(8,128)(2,1)S(1)} all-to-all(f16[8,32,1024]{2,1,0:T(8,128)(2,1)S(1)} %multiply_convert_fusion), channel_id=1, replica_groups=mesh['yh'=4,'zl'=4,'zh'=2,'yl'=2,'x'=4,'c'=2] {'yl','x'}, dimensions={0} | all-to-all | bytes 1048576 | tf_op jit(solution)/shard_map/all_to_all | solution.py:37
  29.0 0.7 pack_tokens.1
  29.7 7.1 %all-to-all-start.2 = ((bf16[8,144,128]{2,1,0:T(8,128)(2,1)}), bf16[8,144,128]{2,1,0:T(8,128)(2,1)S(1)}, u32[]{:S(2)}, u32[]{:S(2)}) async-start(bf16[8,144,128]{2,1,0:T(8,128)(2,1)} %get-tuple-element.20), calls=%async_computation.2 | async-start | bytes 589824 | tf_op jit(solution)/shard_map/all_to_all | solution.py:37
  36.8 0.7 collective-permute-start.1
  37.5 9.4 %all-to-all-done.2.own_ref = bf16[8,144,128]{2,1,0:T(8,128)(2,1)S(1)} async-done(((bf16[8,144,128]{2,1,0:T(8,128)(2,1)}), bf16[8,144,128]{2,1,0:T(8,128)(2,1)S(1)}, u32[]{:S(2)}, u32[]{:S(2)}) %all-to-all-start.2) | async-done | bytes 294944 | tf_op jit(solution)/shard_map/all_to_all | solution.py:37
  46.9 0.7 broadcast_in_dim.2
  47.7 4.6 %all-to-all-start.1 = ((bf16[8,16,1024]{2,1,0:T(8,128)(2,1)}), bf16[8,16,1024]{2,1,0:T(8,128)(2,1)S(1)}, u32[]{:S(2)}, u32[]{:S(2)}) async-start(bf16[8,16,1024]{2,1,0:T(8,128)(2,1)} %broadcast_in_dim.2), calls=%async_computation.1 | async-start | bytes 524288 | tf_op jit(solution)/shard_map/all_to_all | solution.py:37
  52.3 5.1 %collective-permute-start.2 = (bf16[8,144,128]{2,1,0:T(8,128)(2,1)S(1)}, bf16[8,144,128]{2,1,0:T(8,128)(2,1)S(1)}, u32[]{:S(2)}, u32[]{:S(2)}) collective-permute-start(bf16[8,144,128]{2,1,0:T(8,128)(2,1)S(1)} %all-to-all-done.2.own_ref), channel_id=1, source_target_pairs={{0,1},{1,0},{2,3},{3,2},{4,5},{5,4},{6,7},{7,6},{8,9},{9,8},{10,11... | collective-permute-start | bytes 884744 | tf_op jit(solution)/shard_map/ppermute | solution.py:263
  57.5 1.9 %collective-permute-start.3 = (f32[16,1,16]{2,1,0:T(1,128)S(1)}, f32[16,1,16]{2,1,0:T(1,128)S(1)}, u32[]{:S(2)}, u32[]{:S(2)}) collective-permute-start(f32[16,1,16]{2,1,0:T(1,128)S(1)} %get-tuple-element.22), channel_id=1, source_target_pairs={{0,1},{1,0},{2,3},{3,2},{4,5},{5,4},{6,7},{7,6},{8,9},{9,8},{10,11... | collective-permute-start | bytes 3080 | tf_op jit(solution)/shard_map/ppermute | solution.py:271
  59.4 1.1 collective-permute-done.3
  60.7 2.8 %query_grads.1 = bf16[256,512]{1,0:T(8,128)(2,1)S(1)} custom-call(bf16[8,16,1024]{2,1,0:T(8,128)(2,1)S(1)} %all-to-all-done.1.inner_ref, bf16[8,144,128]{2,1,0:T(8,128)(2,1)S(1)} %all-to-all-done.2.own_ref, bf16[8,144,128]{2,1,0:T(8,128)(2,1)S(1)} %collective-permute-done.2.other_ref, f32[1,512]{1,0:T(1,128)S(1)} %reshape.28.scale_ref), custom_call_target="tpu_custom_call" | custom-call | tf_op jit(solution)/shard_map/query_grads/pallas_call | solution.py:178
  63.5 15.3 %all_to_all.31.terms_ref = bf16[4,64,512]{2,1,0:T(8,128)(2,1)S(1)} all-to-all(bf16[4,64,512]{2,1,0:T(8,128)(2,1)S(1)} %bitcast.7), channel_id=1, replica_groups=mesh['yh'=4,'zl'=4,'zh'=2,'yl'=2,'x'=4,'c'=2] {'yh'}, dimensions={0} | all-to-all | bytes 524288 | tf_op jit(solution)/shard_map/all_to_all | solution.py:37
  78.8 0.8 spread_share.1
  79.6 6.1 %all-to-all-start.4 = ((bf16[8,64,512]{2,1,0:T(8,128)(2,1)}), bf16[8,64,512]{2,1,0:T(8,128)(2,1)S(1)}, u32[]{:S(2)}, u32[]{:S(2)}) async-start(bf16[8,64,512]{2,1,0:T(8,128)(2,1)} %spread_share.1), calls=%async_computation.4 | async-start | bytes 1048576 | tf_op jit(solution)/shard_map/all_to_all | solution.py:37
  85.8 1.2 store_levels.1
  87.0 2.8 %collective-permute-start.6 = (bf16[2,2,256,128]{3,2,1,0:T(8,128)(2,1)S(1)}, bf16[2,2,256,128]{3,2,1,0:T(8,128)(2,1)S(1)}, u32[]{:S(2)}, u32[]{:S(2)}) collective-permute-start(bf16[2,2,256,128]{3,2,1,0:T(8,128)(2,1)S(1)} %get-tuple-element.26), channel_id=1, source_target_pairs={{0,96},{32,64},{64,32},{96,0},{1,97},{33,65},{65,33},{97,1},{2,98}... | collective-permute-start | bytes 786440 | tf_op jit(solution)/shard_map/ppermute | solution.py:267
  89.8 3.9 %collective-permute-start.5 = (bf16[2,2,256,128]{3,2,1,0:T(8,128)(2,1)S(1)}, bf16[2,2,256,128]{3,2,1,0:T(8,128)(2,1)S(1)}, u32[]{:S(2)}, u32[]{:S(2)}) collective-permute-start(bf16[2,2,256,128]{3,2,1,0:T(8,128)(2,1)S(1)} %get-tuple-element.25), channel_id=1, source_target_pairs={{0,64},{32,96},{64,0},{96,32},{1,65},{33,97},{65,1},{97,33},{2,66}... | collective-permute-start | bytes 786440 | tf_op jit(solution)/shard_map/ppermute | solution.py:267
  93.7 4.7 %collective-permute-start.4 = (bf16[2,2,256,128]{3,2,1,0:T(8,128)(2,1)S(1)}, bf16[2,2,256,128]{3,2,1,0:T(8,128)(2,1)S(1)}, u32[]{:S(2)}, u32[]{:S(2)}) collective-permute-start(bf16[2,2,256,128]{3,2,1,0:T(8,128)(2,1)S(1)} %get-tuple-element.24), channel_id=1, source_target_pairs={{0,32},{32,0},{64,96},{96,64},{1,33},{33,1},{65,97},{97,65},{2,34}... | collective-permute-start | bytes 786440 | tf_op jit(solution)/shard_map/ppermute | solution.py:267
  98.4 6.6 %collective-permute-done.6.refs_3_ = bf16[2,2,256,128]{3,2,1,0:T(8,128)(2,1)S(1)} collective-permute-done((bf16[2,2,256,128]{3,2,1,0:T(8,128)(2,1)S(1)}, bf16[2,2,256,128]{3,2,1,0:T(8,128)(2,1)S(1)}, u32[]{:S(2)}, u32[]{:S(2)}) %collective-permute-start.6) | collective-permute-done | bytes 262176 | tf_op jit(solution)/shard_map/ppermute | solution.py:267
  105.0 6.8 %collective-permute-done.5.refs_2_ = bf16[2,2,256,128]{3,2,1,0:T(8,128)(2,1)S(1)} collective-permute-done((bf16[2,2,256,128]{3,2,1,0:T(8,128)(2,1)S(1)}, bf16[2,2,256,128]{3,2,1,0:T(8,128)(2,1)S(1)}, u32[]{:S(2)}, u32[]{:S(2)}) %collective-permute-start.5) | collective-permute-done | bytes 262176 | tf_op jit(solution)/shard_map/ppermute | solution.py:267
  111.8 9.1 %collective-permute-done.4.refs_1_ = bf16[2,2,256,128]{3,2,1,0:T(8,128)(2,1)S(1)} collective-permute-done((bf16[2,2,256,128]{3,2,1,0:T(8,128)(2,1)S(1)}, bf16[2,2,256,128]{3,2,1,0:T(8,128)(2,1)S(1)}, u32[]{:S(2)}, u32[]{:S(2)}) %collective-permute-start.4) | collective-permute-done | bytes 262176 | tf_op jit(solution)/shard_map/ppermute | solution.py:267
  121.0 4.4 %collective-permute-start.7 = (bf16[4,2,256,128]{3,2,1,0:T(8,128)(2,1)S(1)}, bf16[4,2,256,128]{3,2,1,0:T(8,128)(2,1)S(1)}, u32[]{:S(2)}, u32[]{:S(2)}) collective-permute-start(bf16[4,2,256,128]{3,2,1,0:T(8,128)(2,1)S(1)} %pad_maximum_fusion), channel_id=1, source_target_pairs={{0,1},{1,0},{2,3},{3,2},{4,5},{5,4},{6,7},{7,6},{8,9},{9,8},{10,11... | collective-permute-start | bytes 1572872 | tf_op jit(solution)/shard_map/ppermute | solution.py:268
  126.0 1.0 collective-permute-done.7.other_ref
  127.0 1.3 score_terms.1
  128.3 2.3 %collective-permute-start.8 = (f32[4,8,16,128]{3,2,1,0:T(8,128)S(1)}, f32[4,8,16,128]{3,2,1,0:T(8,128)S(1)}, u32[]{:S(2)}, u32[]{:S(2)}) collective-permute-start(f32[4,8,16,128]{3,2,1,0:T(8,128)S(1)} %get-tuple-element.28), channel_id=1, source_target_pairs={{0,1},{1,0},{2,3},{3,2},{4,5},{5,4},{6,7},{7,6},{8,9},{9,8},{10,11... | collective-permute-start | bytes 786440 | tf_op jit(solution)/shard_map/ppermute | solution.py:280
  130.6 1.1 collective-permute-done.8
  131.8 19.1 %all_to_all.32 = bf16[32,16,128]{2,1,0:T(8,128)(2,1)S(1)} all-to-all(bf16[32,16,128]{2,1,0:T(8,128)(2,1)S(1)} %bitcast.10), channel_id=1, replica_groups=mesh['yh'=4,'zl'=4,'zh'=2,'yl'=2,'x'=4,'c'=2] {'zl','yl','x'}, dimensions={0} | all-to-all | bytes 262144 | tf_op jit(solution)/shard_map/all_to_all | solution.py:37
  150.9 0.6 convert_reduce_fusion.1
  (24 shorter events, 1.0 us)
Async XLA Ops:
  5.0 11.2 %collective-permute-start = (f32[8,32,1024]{2,1,0:T(8,128)}, f32[8,32,1024]{2,1,0:T(8,128)S(1)}, u32[]{:S(2)}, u32[]{:S(2)}) collective-permute-start(f32[8,32,1024]{2,1,0:T(8,128)} %get-tuple-element.18), channel_id=1, source_target_pairs={{0,1},{1,0},{2,3},{3,2},{4,5},{5,4},{6,7},{7,6},{8,9},{9,8},{10,11... | collective-permute-start | bytes 3145736 | tf_op jit(solution)/shard_map/ppermute | solution.py:253
  16.2 12.8 %copy-start.2 = (s32[1024]{0:T(1024)S(1)}, s32[1024]{0:T(1024)}, u32[]{:S(2)}) copy-start(s32[1024]{0:T(1024)} %param.12) | copy-start | bytes 12292
  17.7 39.7 %copy-start.3 = (f32[4096]{0:T(1024)S(1)}, f32[4096]{0:T(1024)}, u32[]{:S(2)}) copy-start(f32[4096]{0:T(1024)} %param.15) | copy-start | bytes 49156
  29.7 17.2 %all-to-all-start.2 = ((bf16[8,144,128]{2,1,0:T(8,128)(2,1)}), bf16[8,144,128]{2,1,0:T(8,128)(2,1)S(1)}, u32[]{:S(2)}, u32[]{:S(2)}) async-start(bf16[8,144,128]{2,1,0:T(8,128)(2,1)} %get-tuple-element.20), calls=%async_computation.2 | async-start | bytes 589824 | tf_op jit(solution)/shard_map/all_to_all | solution.py:37
  36.8 0.7 collective-permute-start.1
  47.7 38.1 %copy-start = (s32[128,4096]{1,0:T(8,128)S(1)}, s32[128,4096]{1,0:T(8,128)}, u32[]{:S(2)}) copy-start(s32[128,4096]{1,0:T(8,128)} %codes_ref.1) | copy-start | bytes 6291460
  47.7 38.1 %copy-start.1 = (s32[4096]{0:T(1024)S(1)}, s32[4096]{0:T(1024)}, u32[]{:S(2)}) copy-start(s32[4096]{0:T(1024)} %param.14) | copy-start | bytes 49156
  47.7 13.0 %all-to-all-start.1 = ((bf16[8,16,1024]{2,1,0:T(8,128)(2,1)}), bf16[8,16,1024]{2,1,0:T(8,128)(2,1)S(1)}, u32[]{:S(2)}, u32[]{:S(2)}) async-start(bf16[8,16,1024]{2,1,0:T(8,128)(2,1)} %broadcast_in_dim.2), calls=%async_computation.1 | async-start | bytes 524288 | tf_op jit(solution)/shard_map/all_to_all | solution.py:37
  52.3 8.4 %collective-permute-start.2 = (bf16[8,144,128]{2,1,0:T(8,128)(2,1)S(1)}, bf16[8,144,128]{2,1,0:T(8,128)(2,1)S(1)}, u32[]{:S(2)}, u32[]{:S(2)}) collective-permute-start(bf16[8,144,128]{2,1,0:T(8,128)(2,1)S(1)} %all-to-all-done.2.own_ref), channel_id=1, source_target_pairs={{0,1},{1,0},{2,3},{3,2},{4,5},{5,4},{6,7},{7,6},{8,9},{9,8},{10,11... | collective-permute-start | bytes 884744 | tf_op jit(solution)/shard_map/ppermute | solution.py:263
  57.5 3.1 %collective-permute-start.3 = (f32[16,1,16]{2,1,0:T(1,128)S(1)}, f32[16,1,16]{2,1,0:T(1,128)S(1)}, u32[]{:S(2)}, u32[]{:S(2)}) collective-permute-start(f32[16,1,16]{2,1,0:T(1,128)S(1)} %get-tuple-element.22), channel_id=1, source_target_pairs={{0,1},{1,0},{2,3},{3,2},{4,5},{5,4},{6,7},{7,6},{8,9},{9,8},{10,11... | collective-permute-start | bytes 3080 | tf_op jit(solution)/shard_map/ppermute | solution.py:271
  79.6 47.3 %all-to-all-start.4 = ((bf16[8,64,512]{2,1,0:T(8,128)(2,1)}), bf16[8,64,512]{2,1,0:T(8,128)(2,1)S(1)}, u32[]{:S(2)}, u32[]{:S(2)}) async-start(bf16[8,64,512]{2,1,0:T(8,128)(2,1)} %spread_share.1), calls=%async_computation.4 | async-start | bytes 1048576 | tf_op jit(solution)/shard_map/all_to_all | solution.py:37
  87.0 18.0 %collective-permute-start.6 = (bf16[2,2,256,128]{3,2,1,0:T(8,128)(2,1)S(1)}, bf16[2,2,256,128]{3,2,1,0:T(8,128)(2,1)S(1)}, u32[]{:S(2)}, u32[]{:S(2)}) collective-permute-start(bf16[2,2,256,128]{3,2,1,0:T(8,128)(2,1)S(1)} %get-tuple-element.26), channel_id=1, source_target_pairs={{0,96},{32,64},{64,32},{96,0},{1,97},{33,65},{65,33},{97,1},{2,98}... | collective-permute-start | bytes 786440 | tf_op jit(solution)/shard_map/ppermute | solution.py:267
  89.8 22.0 %collective-permute-start.5 = (bf16[2,2,256,128]{3,2,1,0:T(8,128)(2,1)S(1)}, bf16[2,2,256,128]{3,2,1,0:T(8,128)(2,1)S(1)}, u32[]{:S(2)}, u32[]{:S(2)}) collective-permute-start(bf16[2,2,256,128]{3,2,1,0:T(8,128)(2,1)S(1)} %get-tuple-element.25), channel_id=1, source_target_pairs={{0,64},{32,96},{64,0},{96,32},{1,65},{33,97},{65,1},{97,33},{2,66}... | collective-permute-start | bytes 786440 | tf_op jit(solution)/shard_map/ppermute | solution.py:267
  93.7 27.2 %collective-permute-start.4 = (bf16[2,2,256,128]{3,2,1,0:T(8,128)(2,1)S(1)}, bf16[2,2,256,128]{3,2,1,0:T(8,128)(2,1)S(1)}, u32[]{:S(2)}, u32[]{:S(2)}) collective-permute-start(bf16[2,2,256,128]{3,2,1,0:T(8,128)(2,1)S(1)} %get-tuple-element.24), channel_id=1, source_target_pairs={{0,32},{32,0},{64,96},{96,64},{1,33},{33,1},{65,97},{97,65},{2,34}... | collective-permute-start | bytes 786440 | tf_op jit(solution)/shard_map/ppermute | solution.py:267
  121.0 6.0 %collective-permute-start.7 = (bf16[4,2,256,128]{3,2,1,0:T(8,128)(2,1)S(1)}, bf16[4,2,256,128]{3,2,1,0:T(8,128)(2,1)S(1)}, u32[]{:S(2)}, u32[]{:S(2)}) collective-permute-start(bf16[4,2,256,128]{3,2,1,0:T(8,128)(2,1)S(1)} %pad_maximum_fusion), channel_id=1, source_target_pairs={{0,1},{1,0},{2,3},{3,2},{4,5},{5,4},{6,7},{7,6},{8,9},{9,8},{10,11... | collective-permute-start | bytes 1572872 | tf_op jit(solution)/shard_map/ppermute | solution.py:268
  128.3 3.4 %collective-permute-start.8 = (f32[4,8,16,128]{3,2,1,0:T(8,128)S(1)}, f32[4,8,16,128]{3,2,1,0:T(8,128)S(1)}, u32[]{:S(2)}, u32[]{:S(2)}) collective-permute-start(f32[4,8,16,128]{3,2,1,0:T(8,128)S(1)} %get-tuple-element.28), channel_id=1, source_target_pairs={{0,1},{1,0},{2,3},{3,2},{4,5},{5,4},{6,7},{7,6},{8,9},{9,8},{10,11... | collective-permute-start | bytes 786440 | tf_op jit(solution)/shard_map/ppermute | solution.py:280
where the time goes:
time: 152 us; the launch traced here: 151 us
  starting transfers between devices  52.3 us (34%)
  blocking collectives  45.6 us (30%)
  waiting for transfers between devices  37.7 us (25%)
  Pallas kernels  12.4 us (8%)
  other arithmetic  2.34 us (2%)
    all_to_all x3, blocking collectives, exchange(): return lax.all_to_all(blocks, axes, 0, 0, tiled=True)  45.6 us
    ppermute x3, waiting for transfers between devices, local(): store[k] = lax.ppermute(store[k], 'zl', [(r, r ^ k) for r in range(ZL)])  22.5 us
    all_to_all x3, starting transfers between devices, exchange(): return lax.all_to_all(blocks, axes, 0, 0, tiled=True)  17.9 us
    ppermute x3, starting transfers between devices, local(): store[k] = lax.ppermute(store[k], 'zl', [(r, r ^ k) for r in range(ZL)])  11.4 us
    ppermute x2, starting transfers between devices, local(): got = lax.ppermute(send, 'c', flip)  11 us
    all_to_all x3, waiting for transfers between devices, exchange(): return lax.all_to_all(blocks, axes, 0, 0, tiled=True)  9.42 us
    ppermute x1, starting transfers between devices, local(): other = lax.ppermute(own, 'c', flip)  5.06 us
    pallas_call x1, Pallas kernels, project(): pl.pallas_call(project_kernel, grid=(tokens // span,), in_specs=[wide, wi...  5 us
  transfers between devices with their start and end apart: 12, of which 8 were waited for; matrix products, arithmetic and copies ran while one was open for 0% of the time, Pallas kernels for 1%

commit v1 on v0

--- a/solution.py
+++ b/solution.py
@@ -86,18 +86,10 @@
     )(scales.reshape(NI, NF, NJ))
 
 
-def project_kernel(acts_ref, grads_ref, in_ref, out_ref, keep_ref, send_ref, turned, full):
+def project_kernel(acts_ref, grads_ref, in_ref, out_ref, keep_ref, send_ref, full):
     c = lax.axis_index("c")
-
-    @pl.when(pl.program_id(0) == 0)
-    def turn():
-        turned[0] = in_ref[...].T
-        turned[1] = out_ref[...].T
-
-    for side, ref in enumerate((acts_ref, grads_ref)):
-        full[side] = lax.dot_general(
-            turned[side], ref[...], (((1,), (1,)), ((), ())), preferred_element_type=f32
-        )
+    for side, (rows_ref, proj_ref) in enumerate(((acts_ref, in_ref), (grads_ref, out_ref))):
+        full[side] = jnp.dot(rows_ref[...], proj_ref[...], preferred_element_type=f32).T
     for w in range(NW):
         for ref, core in ((keep_ref, c), (send_ref, 1 - c)):
             rows = pl.ds(pl.multiple_of((core * NZ + w) * NJ, NJ), NJ)
@@ -108,7 +100,7 @@
 
 def project(acts, out_grads, proj_in, proj_out):
     tokens, depth = acts.shape
-    span = 2 * LANES
+    span = 4 * LANES
     wide = pl.BlockSpec((span, depth), lambda g: (g, 0))
     whole = pl.BlockSpec((depth, RANK), lambda g: (0, 0))
     shape = jax.ShapeDtypeStruct((NW, NJ + NI, tokens), f32)
@@ -118,7 +110,7 @@
         in_specs=[wide, wide, whole, whole],
         out_specs=[pl.BlockSpec((NW, NJ + NI, span), lambda g: (0, 0, g))] * 2,
         out_shape=[shape] * 2,
-        scratch_shapes=[pltpu.VMEM((2, RANK, depth), bf16), pltpu.VMEM((2, RANK, span), f32)],
+        scratch_shapes=[pltpu.VMEM((2, RANK, span), f32)],
         name="project",
     )(acts, out_grads, proj_in, proj_out)
 

time: 152 us -> 152 us (level)
  no operation moved by 1% of the time
where the time goes in v1:
time: 152 us; the launch traced here: 151 us
  starting transfers between devices  52.3 us (34%)
  blocking collectives  45.5 us (30%)
  waiting for transfers between devices  37.7 us (25%)
  Pallas kernels  11.7 us (8%)
  other arithmetic  2.34 us (2%)
    all_to_all x3, blocking collectives, exchange(): return lax.all_to_all(blocks, axes, 0, 0, tiled=True)  45.5 us
    ppermute x3, waiting for transfers between devices, local(): store[k] = lax.ppermute(store[k], 'zl', [(r, r ^ k) for r in range(ZL)])  22.5 us
    all_to_all x3, starting transfers between devices, exchange(): return lax.all_to_all(blocks, axes, 0, 0, tiled=True)  17.9 us
    ppermute x3, starting transfers between devices, local(): store[k] = lax.ppermute(store[k], 'zl', [(r, r ^ k) for r in range(ZL)])  11.4 us
    ppermute x2, starting transfers between devices, local(): got = lax.ppermute(send, 'c', flip)  11 us
    all_to_all x3, waiting for transfers between devices, exchange(): return lax.all_to_all(blocks, axes, 0, 0, tiled=True)  9.42 us
    ppermute x1, starting transfers between devices, local(): other = lax.ppermute(own, 'c', flip)  5.06 us
    ppermute x1, starting transfers between devices, local(): lax.ppermute(jnp.stack([block[1] for block in store]), 'c', flip)  4.44 us
  transfers between devices with their start and end apart: 12, of which 8 were waited for; matrix products, arithmetic and copies ran while one was open for 0% of the time, Pallas kernels for 1%

profile of v1, /device:TPU:1, one launch (start us, length us, event | category | flops | bytes accessed | tf_op | source)
XLA Modules:
  0.0 150.7 jit_solution(9104663487394654385)
XLA Ops:
  0.0 4.2 %project.1 = (f32[8,32,1024]{2,1,0:T(8,128)}, f32[8,32,1024]{2,1,0:T(8,128)}) custom-call(bf16[1024,512]{1,0:T(8,128)(2,1)} %acts_ref.1, bf16[1024,512]{1,0:T(8,128)(2,1)} %grads_ref.1, bf16[512,256]{1,0:T(8,128)(2,1)} %in_ref.1, bf16[512,256]{1,0:T(8,128)(2,1)} %out_ref.1), custom_call_target="tpu_custom_call" | custom-call | tf_op jit(solution)/shard_map/project/pallas_call | solution.py:107
  4.2 8.7 %collective-permute-start = (f32[8,32,1024]{2,1,0:T(8,128)}, f32[8,32,1024]{2,1,0:T(8,128)S(1)}, u32[]{:S(2)}, u32[]{:S(2)}) collective-permute-start(f32[8,32,1024]{2,1,0:T(8,128)} %get-tuple-element.18), channel_id=1, source_target_pairs={{0,1},{1,0},{2,3},{3,2},{4,5},{5,4},{6,7},{7,6},{8,9},{9,8},{10,11... | collective-permute-start | bytes 3145736 | tf_op jit(solution)/shard_map/ppermute | solution.py:245
  12.9 2.5 %collective-permute-done = f32[8,32,1024]{2,1,0:T(8,128)S(1)} collective-permute-done((f32[8,32,1024]{2,1,0:T(8,128)}, f32[8,32,1024]{2,1,0:T(8,128)S(1)}, u32[]{:S(2)}, u32[]{:S(2)}) %collective-permute-start) | collective-permute-done | bytes 1048608 | tf_op jit(solution)/shard_map/ppermute | solution.py:245
  15.4 1.5 multiply_convert_fusion
  16.9 11.2 %all_to_all.30 = f16[8,32,1024]{2,1,0:T(8,128)(2,1)S(1)} all-to-all(f16[8,32,1024]{2,1,0:T(8,128)(2,1)S(1)} %multiply_convert_fusion), channel_id=1, replica_groups=mesh['yh'=4,'zl'=4,'zh'=2,'yl'=2,'x'=4,'c'=2] {'yl','x'}, dimensions={0} | all-to-all | bytes 1048576 | tf_op jit(solution)/shard_map/all_to_all | solution.py:37
  28.2 0.7 pack_tokens.1
  28.9 7.1 %all-to-all-start.2 = ((bf16[8,144,128]{2,1,0:T(8,128)(2,1)}), bf16[8,144,128]{2,1,0:T(8,128)(2,1)S(1)}, u32[]{:S(2)}, u32[]{:S(2)}) async-start(bf16[8,144,128]{2,1,0:T(8,128)(2,1)} %get-tuple-element.20), calls=%async_computation.2 | async-start | bytes 589824 | tf_op jit(solution)/shard_map/all_to_all | solution.py:37
  36.0 0.7 collective-permute-start.1
  36.7 9.4 %all-to-all-done.2.own_ref = bf16[8,144,128]{2,1,0:T(8,128)(2,1)S(1)} async-done(((bf16[8,144,128]{2,1,0:T(8,128)(2,1)}), bf16[8,144,128]{2,1,0:T(8,128)(2,1)S(1)}, u32[]{:S(2)}, u32[]{:S(2)}) %all-to-all-start.2) | async-done | bytes 294944 | tf_op jit(solution)/shard_map/all_to_all | solution.py:37
  46.1 0.7 broadcast_in_dim.2
  46.9 4.6 %all-to-all-start.1 = ((bf16[8,16,1024]{2,1,0:T(8,128)(2,1)}), bf16[8,16,1024]{2,1,0:T(8,128)(2,1)S(1)}, u32[]{:S(2)}, u32[]{:S(2)}) async-start(bf16[8,16,1024]{2,1,0:T(8,128)(2,1)} %broadcast_in_dim.2), calls=%async_computation.1 | async-start | bytes 524288 | tf_op jit(solution)/shard_map/all_to_all | solution.py:37
  51.5 5.1 %collective-permute-start.2 = (bf16[8,144,128]{2,1,0:T(8,128)(2,1)S(1)}, bf16[8,144,128]{2,1,0:T(8,128)(2,1)S(1)}, u32[]{:S(2)}, u32[]{:S(2)}) collective-permute-start(bf16[8,144,128]{2,1,0:T(8,128)(2,1)S(1)} %all-to-all-done.2.own_ref), channel_id=1, source_target_pairs={{0,1},{1,0},{2,3},{3,2},{4,5},{5,4},{6,7},{7,6},{8,9},{9,8},{10,11... | collective-permute-start | bytes 884744 | tf_op jit(solution)/shard_map/ppermute | solution.py:255
  56.7 1.9 %collective-permute-start.3 = (f32[16,1,16]{2,1,0:T(1,128)S(1)}, f32[16,1,16]{2,1,0:T(1,128)S(1)}, u32[]{:S(2)}, u32[]{:S(2)}) collective-permute-start(f32[16,1,16]{2,1,0:T(1,128)S(1)} %get-tuple-element.22), channel_id=1, source_target_pairs={{0,1},{1,0},{2,3},{3,2},{4,5},{5,4},{6,7},{7,6},{8,9},{9,8},{10,11... | collective-permute-start | bytes 3080 | tf_op jit(solution)/shard_map/ppermute | solution.py:263
  58.6 1.1 collective-permute-done.3
  59.9 2.8 %query_grads.1 = bf16[256,512]{1,0:T(8,128)(2,1)S(1)} custom-call(bf16[8,16,1024]{2,1,0:T(8,128)(2,1)S(1)} %all-to-all-done.1.inner_ref, bf16[8,144,128]{2,1,0:T(8,128)(2,1)S(1)} %all-to-all-done.2.own_ref, bf16[8,144,128]{2,1,0:T(8,128)(2,1)S(1)} %collective-permute-done.2.other_ref, f32[1,512]{1,0:T(1,128)S(1)} %reshape.28.scale_ref), custom_call_target="tpu_custom_call" | custom-call | tf_op jit(solution)/shard_map/query_grads/pallas_call | solution.py:170
  62.7 15.3 %all_to_all.31.terms_ref = bf16[4,64,512]{2,1,0:T(8,128)(2,1)S(1)} all-to-all(bf16[4,64,512]{2,1,0:T(8,128)(2,1)S(1)} %bitcast.7), channel_id=1, replica_groups=mesh['yh'=4,'zl'=4,'zh'=2,'yl'=2,'x'=4,'c'=2] {'yh'}, dimensions={0} | all-to-all | bytes 524288 | tf_op jit(solution)/shard_map/all_to_all | solution.py:37
  78.0 0.8 spread_share.1
  78.8 6.1 %all-to-all-start.4 = ((bf16[8,64,512]{2,1,0:T(8,128)(2,1)}), bf16[8,64,512]{2,1,0:T(8,128)(2,1)S(1)}, u32[]{:S(2)}, u32[]{:S(2)}) async-start(bf16[8,64,512]{2,1,0:T(8,128)(2,1)} %spread_share.1), calls=%async_computation.4 | async-start | bytes 1048576 | tf_op jit(solution)/shard_map/all_to_all | solution.py:37
  85.0 1.2 store_levels.1
  86.2 2.8 %collective-permute-start.6 = (bf16[2,2,256,128]{3,2,1,0:T(8,128)(2,1)S(1)}, bf16[2,2,256,128]{3,2,1,0:T(8,128)(2,1)S(1)}, u32[]{:S(2)}, u32[]{:S(2)}) collective-permute-start(bf16[2,2,256,128]{3,2,1,0:T(8,128)(2,1)S(1)} %get-tuple-element.26), channel_id=1, source_target_pairs={{0,96},{32,64},{64,32},{96,0},{1,97},{33,65},{65,33},{97,1},{2,98}... | collective-permute-start | bytes 786440 | tf_op jit(solution)/shard_map/ppermute | solution.py:259
  89.0 3.9 %collective-permute-start.5 = (bf16[2,2,256,128]{3,2,1,0:T(8,128)(2,1)S(1)}, bf16[2,2,256,128]{3,2,1,0:T(8,128)(2,1)S(1)}, u32[]{:S(2)}, u32[]{:S(2)}) collective-permute-start(bf16[2,2,256,128]{3,2,1,0:T(8,128)(2,1)S(1)} %get-tuple-element.25), channel_id=1, source_target_pairs={{0,64},{32,96},{64,0},{96,32},{1,65},{33,97},{65,1},{97,33},{2,66}... | collective-permute-start | bytes 786440 | tf_op jit(solution)/shard_map/ppermute | solution.py:259
  92.9 4.7 %collective-permute-start.4 = (bf16[2,2,256,128]{3,2,1,0:T(8,128)(2,1)S(1)}, bf16[2,2,256,128]{3,2,1,0:T(8,128)(2,1)S(1)}, u32[]{:S(2)}, u32[]{:S(2)}) collective-permute-start(bf16[2,2,256,128]{3,2,1,0:T(8,128)(2,1)S(1)} %get-tuple-element.24), channel_id=1, source_target_pairs={{0,32},{32,0},{64,96},{96,64},{1,33},{33,1},{65,97},{97,65},{2,34}... | collective-permute-start | bytes 786440 | tf_op jit(solution)/shard_map/ppermute | solution.py:259
  97.6 6.6 %collective-permute-done.6.refs_3_ = bf16[2,2,256,128]{3,2,1,0:T(8,128)(2,1)S(1)} collective-permute-done((bf16[2,2,256,128]{3,2,1,0:T(8,128)(2,1)S(1)}, bf16[2,2,256,128]{3,2,1,0:T(8,128)(2,1)S(1)}, u32[]{:S(2)}, u32[]{:S(2)}) %collective-permute-start.6) | collective-permute-done | bytes 262176 | tf_op jit(solution)/shard_map/ppermute | solution.py:259
  104.2 6.8 %collective-permute-done.5.refs_2_ = bf16[2,2,256,128]{3,2,1,0:T(8,128)(2,1)S(1)} collective-permute-done((bf16[2,2,256,128]{3,2,1,0:T(8,128)(2,1)S(1)}, bf16[2,2,256,128]{3,2,1,0:T(8,128)(2,1)S(1)}, u32[]{:S(2)}, u32[]{:S(2)}) %collective-permute-start.5) | collective-permute-done | bytes 262176 | tf_op jit(solution)/shard_map/ppermute | solution.py:259
  111.0 9.1 %collective-permute-done.4.refs_1_ = bf16[2,2,256,128]{3,2,1,0:T(8,128)(2,1)S(1)} collective-permute-done((bf16[2,2,256,128]{3,2,1,0:T(8,128)(2,1)S(1)}, bf16[2,2,256,128]{3,2,1,0:T(8,128)(2,1)S(1)}, u32[]{:S(2)}, u32[]{:S(2)}) %collective-permute-start.4) | collective-permute-done | bytes 262176 | tf_op jit(solution)/shard_map/ppermute | solution.py:259
  120.2 4.4 %collective-permute-start.7 = (bf16[4,2,256,128]{3,2,1,0:T(8,128)(2,1)S(1)}, bf16[4,2,256,128]{3,2,1,0:T(8,128)(2,1)S(1)}, u32[]{:S(2)}, u32[]{:S(2)}) collective-permute-start(bf16[4,2,256,128]{3,2,1,0:T(8,128)(2,1)S(1)} %pad_maximum_fusion), channel_id=1, source_target_pairs={{0,1},{1,0},{2,3},{3,2},{4,5},{5,4},{6,7},{7,6},{8,9},{9,8},{10,11... | collective-permute-start | bytes 1572872 | tf_op jit(solution)/shard_map/ppermute | solution.py:260
  125.2 1.0 collective-permute-done.7.other_ref
  126.2 1.3 score_terms.1
  127.5 2.3 %collective-permute-start.8 = (f32[4,8,16,128]{3,2,1,0:T(8,128)S(1)}, f32[4,8,16,128]{3,2,1,0:T(8,128)S(1)}, u32[]{:S(2)}, u32[]{:S(2)}) collective-permute-start(f32[4,8,16,128]{3,2,1,0:T(8,128)S(1)} %get-tuple-element.28), channel_id=1, source_target_pairs={{0,1},{1,0},{2,3},{3,2},{4,5},{5,4},{6,7},{7,6},{8,9},{9,8},{10,11... | collective-permute-start | bytes 786440 | tf_op jit(solution)/shard_map/ppermute | solution.py:272
  129.8 1.1 collective-permute-done.8
  131.0 19.0 %all_to_all.32 = bf16[32,16,128]{2,1,0:T(8,128)(2,1)S(1)} all-to-all(bf16[32,16,128]{2,1,0:T(8,128)(2,1)S(1)} %bitcast.10), channel_id=1, replica_groups=mesh['yh'=4,'zl'=4,'zh'=2,'yl'=2,'x'=4,'c'=2] {'zl','yl','x'}, dimensions={0} | all-to-all | bytes 262144 | tf_op jit(solution)/shard_map/all_to_all | solution.py:37
  150.1 0.6 convert_reduce_fusion.1
  (24 shorter events, 1.0 us)
Async XLA Ops:
  4.2 11.2 %collective-permute-start = (f32[8,32,1024]{2,1,0:T(8,128)}, f32[8,32,1024]{2,1,0:T(8,128)S(1)}, u32[]{:S(2)}, u32[]{:S(2)}) collective-permute-start(f32[8,32,1024]{2,1,0:T(8,128)} %get-tuple-element.18), channel_id=1, source_target_pairs={{0,1},{1,0},{2,3},{3,2},{4,5},{5,4},{6,7},{7,6},{8,9},{9,8},{10,11... | collective-permute-start | bytes 3145736 | tf_op jit(solution)/shard_map/ppermute | solution.py:245
  15.4 12.8 %copy-start.2 = (s32[1024]{0:T(1024)S(1)}, s32[1024]{0:T(1024)}, u32[]{:S(2)}) copy-start(s32[1024]{0:T(1024)} %param.12) | copy-start | bytes 12292
  16.8 39.7 %copy-start.3 = (f32[4096]{0:T(1024)S(1)}, f32[4096]{0:T(1024)}, u32[]{:S(2)}) copy-start(f32[4096]{0:T(1024)} %param.15) | copy-start | bytes 49156
  28.9 17.2 %all-to-all-start.2 = ((bf16[8,144,128]{2,1,0:T(8,128)(2,1)}), bf16[8,144,128]{2,1,0:T(8,128)(2,1)S(1)}, u32[]{:S(2)}, u32[]{:S(2)}) async-start(bf16[8,144,128]{2,1,0:T(8,128)(2,1)} %get-tuple-element.20), calls=%async_computation.2 | async-start | bytes 589824 | tf_op jit(solution)/shard_map/all_to_all | solution.py:37
  36.0 0.7 collective-permute-start.1
  46.8 38.1 %copy-start = (s32[128,4096]{1,0:T(8,128)S(1)}, s32[128,4096]{1,0:T(8,128)}, u32[]{:S(2)}) copy-start(s32[128,4096]{1,0:T(8,128)} %codes_ref.1) | copy-start | bytes 6291460
  46.9 38.1 %copy-start.1 = (s32[4096]{0:T(1024)S(1)}, s32[4096]{0:T(1024)}, u32[]{:S(2)}) copy-start(s32[4096]{0:T(1024)} %param.14) | copy-start | bytes 49156
  46.9 13.0 %all-to-all-start.1 = ((bf16[8,16,1024]{2,1,0:T(8,128)(2,1)}), bf16[8,16,1024]{2,1,0:T(8,128)(2,1)S(1)}, u32[]{:S(2)}, u32[]{:S(2)}) async-start(bf16[8,16,1024]{2,1,0:T(8,128)(2,1)} %broadcast_in_dim.2), calls=%async_computation.1 | async-start | bytes 524288 | tf_op jit(solution)/shard_map/all_to_all | solution.py:37
  51.5 8.4 %collective-permute-start.2 = (bf16[8,144,128]{2,1,0:T(8,128)(2,1)S(1)}, bf16[8,144,128]{2,1,0:T(8,128)(2,1)S(1)}, u32[]{:S(2)}, u32[]{:S(2)}) collective-permute-start(bf16[8,144,128]{2,1,0:T(8,128)(2,1)S(1)} %all-to-all-done.2.own_ref), channel_id=1, source_target_pairs={{0,1},{1,0},{2,3},{3,2},{4,5},{5,4},{6,7},{7,6},{8,9},{9,8},{10,11... | collective-permute-start | bytes 884744 | tf_op jit(solution)/shard_map/ppermute | solution.py:255
  56.7 3.1 %collective-permute-start.3 = (f32[16,1,16]{2,1,0:T(1,128)S(1)}, f32[16,1,16]{2,1,0:T(1,128)S(1)}, u32[]{:S(2)}, u32[]{:S(2)}) collective-permute-start(f32[16,1,16]{2,1,0:T(1,128)S(1)} %get-tuple-element.22), channel_id=1, source_target_pairs={{0,1},{1,0},{2,3},{3,2},{4,5},{5,4},{6,7},{7,6},{8,9},{9,8},{10,11... | collective-permute-start | bytes 3080 | tf_op jit(solution)/shard_map/ppermute | solution.py:263
  78.8 47.4 %all-to-all-start.4 = ((bf16[8,64,512]{2,1,0:T(8,128)(2,1)}), bf16[8,64,512]{2,1,0:T(8,128)(2,1)S(1)}, u32[]{:S(2)}, u32[]{:S(2)}) async-start(bf16[8,64,512]{2,1,0:T(8,128)(2,1)} %spread_share.1), calls=%async_computation.4 | async-start | bytes 1048576 | tf_op jit(solution)/shard_map/all_to_all | solution.py:37
  86.2 18.0 %collective-permute-start.6 = (bf16[2,2,256,128]{3,2,1,0:T(8,128)(2,1)S(1)}, bf16[2,2,256,128]{3,2,1,0:T(8,128)(2,1)S(1)}, u32[]{:S(2)}, u32[]{:S(2)}) collective-permute-start(bf16[2,2,256,128]{3,2,1,0:T(8,128)(2,1)S(1)} %get-tuple-element.26), channel_id=1, source_target_pairs={{0,96},{32,64},{64,32},{96,0},{1,97},{33,65},{65,33},{97,1},{2,98}... | collective-permute-start | bytes 786440 | tf_op jit(solution)/shard_map/ppermute | solution.py:259
  89.0 22.0 %collective-permute-start.5 = (bf16[2,2,256,128]{3,2,1,0:T(8,128)(2,1)S(1)}, bf16[2,2,256,128]{3,2,1,0:T(8,128)(2,1)S(1)}, u32[]{:S(2)}, u32[]{:S(2)}) collective-permute-start(bf16[2,2,256,128]{3,2,1,0:T(8,128)(2,1)S(1)} %get-tuple-element.25), channel_id=1, source_target_pairs={{0,64},{32,96},{64,0},{96,32},{1,65},{33,97},{65,1},{97,33},{2,66}... | collective-permute-start | bytes 786440 | tf_op jit(solution)/shard_map/ppermute | solution.py:259
  92.9 27.2 %collective-permute-start.4 = (bf16[2,2,256,128]{3,2,1,0:T(8,128)(2,1)S(1)}, bf16[2,2,256,128]{3,2,1,0:T(8,128)(2,1)S(1)}, u32[]{:S(2)}, u32[]{:S(2)}) collective-permute-start(bf16[2,2,256,128]{3,2,1,0:T(8,128)(2,1)S(1)} %get-tuple-element.24), channel_id=1, source_target_pairs={{0,32},{32,0},{64,96},{96,64},{1,33},{33,1},{65,97},{97,65},{2,34}... | collective-permute-start | bytes 786440 | tf_op jit(solution)/shard_map/ppermute | solution.py:259
  120.2 6.0 %collective-permute-start.7 = (bf16[4,2,256,128]{3,2,1,0:T(8,128)(2,1)S(1)}, bf16[4,2,256,128]{3,2,1,0:T(8,128)(2,1)S(1)}, u32[]{:S(2)}, u32[]{:S(2)}) collective-permute-start(bf16[4,2,256,128]{3,2,1,0:T(8,128)(2,1)S(1)} %pad_maximum_fusion), channel_id=1, source_target_pairs={{0,1},{1,0},{2,3},{3,2},{4,5},{5,4},{6,7},{7,6},{8,9},{9,8},{10,11... | collective-permute-start | bytes 1572872 | tf_op jit(solution)/shard_map/ppermute | solution.py:260
  127.5 3.4 %collective-permute-start.8 = (f32[4,8,16,128]{3,2,1,0:T(8,128)S(1)}, f32[4,8,16,128]{3,2,1,0:T(8,128)S(1)}, u32[]{:S(2)}, u32[]{:S(2)}) collective-permute-start(f32[4,8,16,128]{3,2,1,0:T(8,128)S(1)} %get-tuple-element.28), channel_id=1, source_target_pairs={{0,1},{1,0},{2,3},{3,2},{4,5},{5,4},{6,7},{7,6},{8,9},{9,8},{10,11... | collective-permute-start | bytes 786440 | tf_op jit(solution)/shard_map/ppermute | solution.py:272

commit v2 on v1

--- a/solution.py
+++ b/solution.py
@@ -23,7 +23,7 @@
 HALF = NI * NJ
 LANES = 128
 OWNER_ROW = 128
-PACKED_ROWS = 144
+PACKED_ROWS = 136
 LINK_GAIN = 128.0
 f32 = jnp.float32
 bf16 = jnp.bfloat16
@@ -120,7 +120,7 @@
     inner_ref[...] = values[:NJ].astype(bf16)
     outer = values[NJ:].astype(bf16)
     owners = owner_ref[...].astype(f32)
-    tail = jnp.concatenate([owners, jnp.zeros_like(owners)], axis=0).astype(bf16)
+    tail = owners.astype(bf16)
     for r in range(NZ):
         for t in range(NZ):
             packed_ref[r, t * NI : (t + 1) * NI, :] = outer[:, t * LANES : (t + 1) * LANES]
@@ -162,7 +162,7 @@
             acc[...] += lax.dot_general(product, mine, (((1,), (1,)), ((), ())), preferred_element_type=f32)
         return carry
 
-    lax.fori_loop(0, NZ, row, 0, unroll=4)
+    lax.fori_loop(0, NZ, row, 0, unroll=8)
     out_ref[...] = (acc[...].T * scale_ref[...]).astype(bf16)
 
 
@@ -199,26 +199,22 @@
 
 
 def terms_kernel(late_ref, scaled_ref, other_ref, *refs):
-    own, (keep_ref, send_ref) = refs[:ZL], refs[ZL:]
-    zl, c = late_ref[0], lax.axis_index("c")
+    own, out_ref = refs[:ZL], refs[ZL]
+    zl = late_ref[0]
     for k in range(ZL):
         terms = jnp.zeros((QUERIES, other_ref.shape[3]), f32)
         for h in range(ZH):
             terms += jnp.dot(scaled_ref[h, :, :HALF], own[k][0, h], preferred_element_type=f32)
             terms += jnp.dot(scaled_ref[h, :, HALF:], other_ref[k, h], preferred_element_type=f32)
-        terms = terms.reshape(NW, 2, QUERIES // NF, terms.shape[1])
-        first, second = terms[:, 0], terms[:, 1]
-        keep_ref[zl ^ k] = jnp.where(c == 0, first, second)
-        send_ref[zl ^ k] = jnp.where(c == 0, second, first)
+        out_ref[zl ^ k] = terms.astype(bf16).reshape(NF, QUERIES // NF, terms.shape[1])
 
 
 def score_terms(late, scaled, own, other):
-    shape = jax.ShapeDtypeStruct((ZL, NW, QUERIES // NF, other.shape[3]), f32)
     return pl.pallas_call(
         terms_kernel,
         in_specs=[SMEM] + [VMEM] * (2 + ZL),
-        out_specs=[VMEM] * 2,
-        out_shape=[shape, shape],
+        out_specs=VMEM,
+        out_shape=jax.ShapeDtypeStruct((ZL, NF, QUERIES // NF, other.shape[3]), bf16),
         compiler_params=SMALL,
         name="score_terms",
     )(late, scaled, other, *own)
@@ -268,10 +264,8 @@
     grads = exchange(grads.reshape(NY, QUERIES // NY, 2 * HALF), "yh")
     scaled = exchange(spread_share(grads), ("zh", "yh")).reshape(ZH, QUERIES, 2 * HALF)
 
-    keep, send = score_terms(late, scaled, store, store_other)
-    got = lax.ppermute(send, "c", flip)
-    terms = (keep + got).astype(bf16).reshape(ZL * NW, QUERIES // NF, codes.shape[0])
-    terms = exchange(terms, ("zl", "yl", "x"))
+    terms = score_terms(late, scaled, store, store_other)
+    terms = exchange(terms.reshape(ZL * NF, QUERIES // NF, codes.shape[0]), ("zl", "yl", "x", "c"))
     return jnp.sum(terms.astype(f32), axis=0)
 
 

time: 152 us -> 151 us (level)
  waiting for transfers between devices: 37.7 us -> 33.5 us
  blocking collectives: 45.5 us -> 49.3 us
    all_to_all x3, blocking collectives: 45.5 us -> 49.3 us  [exchange(): return lax.all_to_all(blocks, axes, 0, 0, tiled=True)]
    ppermute x1, starting transfers between devices: 4.44 us -> 7.13 us  [local(): lax.ppermute(jnp.stack([block[1] for block in store]), 'c', flip)]
    ppermute x3, waiting for transfers between devices: 22.5 us -> 19.8 us  [local(): store[k] = lax.ppermute(store[k], 'zl', [(r, r ^ k) for r in range(ZL)])]
    ppermute x2 -> x1, starting transfers between devices: 11 us -> 8.69 us  [local(): got = lax.ppermute(send, 'c', flip)]
    ppermute x2 -> x1, waiting for transfers between devices: 3.62 us -> 2.48 us  [local(): got = lax.ppermute(send, 'c', flip)]
  transfers between devices with their start and end apart: 12 -> 11, of which waited for: 8 -> 7; matrix products, arithmetic and copies ran while one was open for 0% -> 0% of each run, Pallas kernels for 1% -> 1%
where the time goes in v2:
time: 151 us; the launch traced here: 150 us
  starting transfers between devices  52.7 us (35%)
  blocking collectives  49.3 us (33%)
  waiting for transfers between devices  33.5 us (22%)
  Pallas kernels  11.3 us (7%)
  other arithmetic  2.33 us (2%)
    all_to_all x3, blocking collectives, exchange(): return lax.all_to_all(blocks, axes, 0, 0, tiled=True)  49.3 us
    ppermute x3, waiting for transfers between devices, local(): store[k] = lax.ppermute(store[k], 'zl', [(r, r ^ k) for r in range(ZL)])  19.8 us
    all_to_all x3, starting transfers between devices, exchange(): return lax.all_to_all(blocks, axes, 0, 0, tiled=True)  18 us
    ppermute x3, starting transfers between devices, local(): store[k] = lax.ppermute(store[k], 'zl', [(r, r ^ k) for r in range(ZL)])  11.4 us
    all_to_all x3, waiting for transfers between devices, exchange(): return lax.all_to_all(blocks, axes, 0, 0, tiled=True)  9.08 us
    ppermute x1, starting transfers between devices, local(): got = lax.ppermute(send, 'c', flip)  8.69 us
    ppermute x1, starting transfers between devices, local(): lax.ppermute(jnp.stack([block[1] for block in store]), 'c', flip)  7.13 us
    ppermute x1, starting transfers between devices, local(): other = lax.ppermute(own, 'c', flip)  4.95 us
  transfers between devices with their start and end apart: 11, of which 7 were waited for; matrix products, arithmetic and copies ran while one was open for 0% of the time, Pallas kernels for 1%

profile of v2, /device:TPU:1, one launch (start us, length us, event | category | flops | bytes accessed | tf_op | source)
XLA Modules:
  0.0 150.4 jit_solution(11057408192853948309)
XLA Ops:
  0.0 4.2 %project.1 = (f32[8,32,1024]{2,1,0:T(8,128)}, f32[8,32,1024]{2,1,0:T(8,128)}) custom-call(bf16[1024,512]{1,0:T(8,128)(2,1)} %acts_ref.1, bf16[1024,512]{1,0:T(8,128)(2,1)} %grads_ref.1, bf16[512,256]{1,0:T(8,128)(2,1)} %in_ref.1, bf16[512,256]{1,0:T(8,128)(2,1)} %out_ref.1), custom_call_target="tpu_custom_call" | custom-call | tf_op jit(solution)/shard_map/project/pallas_call | solution.py:107
  4.2 8.7 %collective-permute-start = (f32[8,32,1024]{2,1,0:T(8,128)}, f32[8,32,1024]{2,1,0:T(8,128)S(1)}, u32[]{:S(2)}, u32[]{:S(2)}) collective-permute-start(f32[8,32,1024]{2,1,0:T(8,128)} %get-tuple-element.16), channel_id=1, source_target_pairs={{0,1},{1,0},{2,3},{3,2},{4,5},{5,4},{6,7},{7,6},{8,9},{9,8},{10,11... | collective-permute-start | bytes 3145736 | tf_op jit(solution)/shard_map/ppermute | solution.py:241
  12.9 2.5 %collective-permute-done = f32[8,32,1024]{2,1,0:T(8,128)S(1)} collective-permute-done((f32[8,32,1024]{2,1,0:T(8,128)}, f32[8,32,1024]{2,1,0:T(8,128)S(1)}, u32[]{:S(2)}, u32[]{:S(2)}) %collective-permute-start) | collective-permute-done | bytes 1048608 | tf_op jit(solution)/shard_map/ppermute | solution.py:241
  15.4 1.5 multiply_convert_fusion
  16.9 11.2 %all_to_all.30 = f16[8,32,1024]{2,1,0:T(8,128)(2,1)S(1)} all-to-all(f16[8,32,1024]{2,1,0:T(8,128)(2,1)S(1)} %multiply_convert_fusion), channel_id=1, replica_groups=mesh['yh'=4,'zl'=4,'zh'=2,'yl'=2,'x'=4,'c'=2] {'yl','x'}, dimensions={0} | all-to-all | bytes 1048576 | tf_op jit(solution)/shard_map/all_to_all | solution.py:37
  28.2 0.7 pack_tokens.1
  28.9 7.1 %all-to-all-start.2 = ((bf16[8,136,128]{2,1,0:T(8,128)(2,1)}), bf16[8,136,128]{2,1,0:T(8,128)(2,1)S(1)}, u32[]{:S(2)}, u32[]{:S(2)}) async-start(bf16[8,136,128]{2,1,0:T(8,128)(2,1)} %get-tuple-element.18), calls=%async_computation.2 | async-start | bytes 557056 | tf_op jit(solution)/shard_map/all_to_all | solution.py:37
  36.1 0.7 collective-permute-start.1
  36.7 9.1 %all-to-all-done.2.own_ref = bf16[8,136,128]{2,1,0:T(8,128)(2,1)S(1)} async-done(((bf16[8,136,128]{2,1,0:T(8,128)(2,1)}), bf16[8,136,128]{2,1,0:T(8,128)(2,1)S(1)}, u32[]{:S(2)}, u32[]{:S(2)}) %all-to-all-start.2) | async-done | bytes 278560 | tf_op jit(solution)/shard_map/all_to_all | solution.py:37
  45.8 0.7 broadcast_in_dim.2
  46.5 4.7 %all-to-all-start.1 = ((bf16[8,16,1024]{2,1,0:T(8,128)(2,1)}), bf16[8,16,1024]{2,1,0:T(8,128)(2,1)S(1)}, u32[]{:S(2)}, u32[]{:S(2)}) async-start(bf16[8,16,1024]{2,1,0:T(8,128)(2,1)} %broadcast_in_dim.2), calls=%async_computation.1 | async-start | bytes 524288 | tf_op jit(solution)/shard_map/all_to_all | solution.py:37
  51.3 4.9 %collective-permute-start.2 = (bf16[8,136,128]{2,1,0:T(8,128)(2,1)S(1)}, bf16[8,136,128]{2,1,0:T(8,128)(2,1)S(1)}, u32[]{:S(2)}, u32[]{:S(2)}) collective-permute-start(bf16[8,136,128]{2,1,0:T(8,128)(2,1)S(1)} %all-to-all-done.2.own_ref), channel_id=1, source_target_pairs={{0,1},{1,0},{2,3},{3,2},{4,5},{5,4},{6,7},{7,6},{8,9},{9,8},{10,11... | collective-permute-start | bytes 835592 | tf_op jit(solution)/shard_map/ppermute | solution.py:251
  56.2 0.1 reshape.27.scales_ref
  56.4 1.9 %collective-permute-start.3 = (f32[16,1,16]{2,1,0:T(1,128)S(1)}, f32[16,1,16]{2,1,0:T(1,128)S(1)}, u32[]{:S(2)}, u32[]{:S(2)}) collective-permute-start(f32[16,1,16]{2,1,0:T(1,128)S(1)} %get-tuple-element.20), channel_id=1, source_target_pairs={{0,1},{1,0},{2,3},{3,2},{4,5},{5,4},{6,7},{7,6},{8,9},{9,8},{10,11... | collective-permute-start | bytes 3080 | tf_op jit(solution)/shard_map/ppermute | solution.py:259
  58.3 1.1 collective-permute-done.3
  59.6 2.4 %query_grads.1 = bf16[256,512]{1,0:T(8,128)(2,1)S(1)} custom-call(bf16[8,16,1024]{2,1,0:T(8,128)(2,1)S(1)} %all-to-all-done.1.inner_ref, bf16[8,136,128]{2,1,0:T(8,128)(2,1)S(1)} %all-to-all-done.2.own_ref, bf16[8,136,128]{2,1,0:T(8,128)(2,1)S(1)} %collective-permute-done.2.other_ref, f32[1,512]{1,0:T(1,128)S(1)} %reshape.28.scale_ref), custom_call_target="tpu_custom_call" | custom-call | tf_op jit(solution)/shard_map/query_grads/pallas_call | solution.py:170
  62.0 15.3 %all_to_all.31.terms_ref = bf16[4,64,512]{2,1,0:T(8,128)(2,1)S(1)} all-to-all(bf16[4,64,512]{2,1,0:T(8,128)(2,1)S(1)} %bitcast.8), channel_id=1, replica_groups=mesh['yh'=4,'zl'=4,'zh'=2,'yl'=2,'x'=4,'c'=2] {'yh'}, dimensions={0} | all-to-all | bytes 524288 | tf_op jit(solution)/shard_map/all_to_all | solution.py:37
  77.3 0.8 spread_share.1
  78.1 6.1 %all-to-all-start.4 = ((bf16[8,64,512]{2,1,0:T(8,128)(2,1)}), bf16[8,64,512]{2,1,0:T(8,128)(2,1)S(1)}, u32[]{:S(2)}, u32[]{:S(2)}) async-start(bf16[8,64,512]{2,1,0:T(8,128)(2,1)} %spread_share.1), calls=%async_computation.4 | async-start | bytes 1048576 | tf_op jit(solution)/shard_map/all_to_all | solution.py:37
  84.3 1.2 store_levels.1
  85.5 3.1 %collective-permute-start.6 = (bf16[2,2,256,128]{3,2,1,0:T(8,128)(2,1)S(1)}, bf16[2,2,256,128]{3,2,1,0:T(8,128)(2,1)S(1)}, u32[]{:S(2)}, u32[]{:S(2)}) collective-permute-start(bf16[2,2,256,128]{3,2,1,0:T(8,128)(2,1)S(1)} %get-tuple-element.24), channel_id=1, source_target_pairs={{0,96},{32,64},{64,32},{96,0},{1,97},{33,65},{65,33},{97,1},{2,98}... | collective-permute-start | bytes 786440 | tf_op jit(solution)/shard_map/ppermute | solution.py:255
  88.6 3.9 %collective-permute-start.5 = (bf16[2,2,256,128]{3,2,1,0:T(8,128)(2,1)S(1)}, bf16[2,2,256,128]{3,2,1,0:T(8,128)(2,1)S(1)}, u32[]{:S(2)}, u32[]{:S(2)}) collective-permute-start(bf16[2,2,256,128]{3,2,1,0:T(8,128)(2,1)S(1)} %get-tuple-element.23), channel_id=1, source_target_pairs={{0,64},{32,96},{64,0},{96,32},{1,65},{33,97},{65,1},{97,33},{2,66}... | collective-permute-start | bytes 786440 | tf_op jit(solution)/shard_map/ppermute | solution.py:255
  92.5 4.3 %collective-permute-start.4 = (bf16[2,2,256,128]{3,2,1,0:T(8,128)(2,1)S(1)}, bf16[2,2,256,128]{3,2,1,0:T(8,128)(2,1)S(1)}, u32[]{:S(2)}, u32[]{:S(2)}) collective-permute-start(bf16[2,2,256,128]{3,2,1,0:T(8,128)(2,1)S(1)} %get-tuple-element.22), channel_id=1, source_target_pairs={{0,32},{32,0},{64,96},{96,64},{1,33},{33,1},{65,97},{97,65},{2,34}... | collective-permute-start | bytes 786440 | tf_op jit(solution)/shard_map/ppermute | solution.py:255
  96.9 3.6 %collective-permute-done.6.refs_3_ = bf16[2,2,256,128]{3,2,1,0:T(8,128)(2,1)S(1)} collective-permute-done((bf16[2,2,256,128]{3,2,1,0:T(8,128)(2,1)S(1)}, bf16[2,2,256,128]{3,2,1,0:T(8,128)(2,1)S(1)}, u32[]{:S(2)}, u32[]{:S(2)}) %collective-permute-start.6) | collective-permute-done | bytes 262176 | tf_op jit(solution)/shard_map/ppermute | solution.py:255
  100.5 10.0 %collective-permute-done.5.refs_2_ = bf16[2,2,256,128]{3,2,1,0:T(8,128)(2,1)S(1)} collective-permute-done((bf16[2,2,256,128]{3,2,1,0:T(8,128)(2,1)S(1)}, bf16[2,2,256,128]{3,2,1,0:T(8,128)(2,1)S(1)}, u32[]{:S(2)}, u32[]{:S(2)}) %collective-permute-start.5) | collective-permute-done | bytes 262176 | tf_op jit(solution)/shard_map/ppermute | solution.py:255
  110.6 6.2 %collective-permute-done.4.refs_1_ = bf16[2,2,256,128]{3,2,1,0:T(8,128)(2,1)S(1)} collective-permute-done((bf16[2,2,256,128]{3,2,1,0:T(8,128)(2,1)S(1)}, bf16[2,2,256,128]{3,2,1,0:T(8,128)(2,1)S(1)}, u32[]{:S(2)}, u32[]{:S(2)}) %collective-permute-start.4) | collective-permute-done | bytes 262176 | tf_op jit(solution)/shard_map/ppermute | solution.py:255
  116.9 7.1 %collective-permute-start.7 = (bf16[4,2,256,128]{3,2,1,0:T(8,128)(2,1)S(1)}, bf16[4,2,256,128]{3,2,1,0:T(8,128)(2,1)S(1)}, u32[]{:S(2)}, u32[]{:S(2)}) collective-permute-start(bf16[4,2,256,128]{3,2,1,0:T(8,128)(2,1)S(1)} %pad_maximum_fusion), channel_id=1, source_target_pairs={{0,1},{1,0},{2,3},{3,2},{4,5},{5,4},{6,7},{7,6},{8,9},{9,8},{10,11... | collective-permute-start | bytes 1572872 | tf_op jit(solution)/shard_map/ppermute | solution.py:256
  124.0 0.5 late_place.1.late_ref
  124.5 1.0 collective-permute-done.7.other_ref
  125.5 1.4 score_terms.1
  126.9 22.8 %all_to_all.32 = bf16[64,16,128]{2,1,0:T(8,128)(2,1)S(1)} all-to-all(bf16[64,16,128]{2,1,0:T(8,128)(2,1)S(1)} %bitcast.7), channel_id=1, replica_groups=mesh['yh'=4,'zl'=4,'zh'=2,'yl'=2,'x'=4,'c'=2] {'zl','yl','x','c'}, dimensions={0} | all-to-all | bytes 524288 | tf_op jit(solution)/shard_map/all_to_all | solution.py:37
  149.7 0.7 convert_reduce_fusion.1
  (21 shorter events, 0.4 us)
Async XLA Ops:
  4.2 11.2 %collective-permute-start = (f32[8,32,1024]{2,1,0:T(8,128)}, f32[8,32,1024]{2,1,0:T(8,128)S(1)}, u32[]{:S(2)}, u32[]{:S(2)}) collective-permute-start(f32[8,32,1024]{2,1,0:T(8,128)} %get-tuple-element.16), channel_id=1, source_target_pairs={{0,1},{1,0},{2,3},{3,2},{4,5},{5,4},{6,7},{7,6},{8,9},{9,8},{10,11... | collective-permute-start | bytes 3145736 | tf_op jit(solution)/shard_map/ppermute | solution.py:241
  15.4 12.8 %copy-start.2 = (s32[1024]{0:T(1024)S(1)}, s32[1024]{0:T(1024)}, u32[]{:S(2)}) copy-start(s32[1024]{0:T(1024)} %param.12) | copy-start | bytes 12292
  16.9 39.4 %copy-start.3 = (f32[4096]{0:T(1024)S(1)}, f32[4096]{0:T(1024)}, u32[]{:S(2)}) copy-start(f32[4096]{0:T(1024)} %param.15) | copy-start | bytes 49156
  28.9 16.9 %all-to-all-start.2 = ((bf16[8,136,128]{2,1,0:T(8,128)(2,1)}), bf16[8,136,128]{2,1,0:T(8,128)(2,1)S(1)}, u32[]{:S(2)}, u32[]{:S(2)}) async-start(bf16[8,136,128]{2,1,0:T(8,128)(2,1)} %get-tuple-element.18), calls=%async_computation.2 | async-start | bytes 557056 | tf_op jit(solution)/shard_map/all_to_all | solution.py:37
  36.1 0.7 collective-permute-start.1
  46.5 37.7 %copy-start = (s32[128,4096]{1,0:T(8,128)S(1)}, s32[128,4096]{1,0:T(8,128)}, u32[]{:S(2)}) copy-start(s32[128,4096]{1,0:T(8,128)} %codes_ref.1) | copy-start | bytes 6291460
  46.5 37.7 %copy-start.1 = (s32[4096]{0:T(1024)S(1)}, s32[4096]{0:T(1024)}, u32[]{:S(2)}) copy-start(s32[4096]{0:T(1024)} %param.14) | copy-start | bytes 49156
  46.5 13.0 %all-to-all-start.1 = ((bf16[8,16,1024]{2,1,0:T(8,128)(2,1)}), bf16[8,16,1024]{2,1,0:T(8,128)(2,1)S(1)}, u32[]{:S(2)}, u32[]{:S(2)}) async-start(bf16[8,16,1024]{2,1,0:T(8,128)(2,1)} %broadcast_in_dim.2), calls=%async_computation.1 | async-start | bytes 524288 | tf_op jit(solution)/shard_map/all_to_all | solution.py:37
  51.3 8.3 %collective-permute-start.2 = (bf16[8,136,128]{2,1,0:T(8,128)(2,1)S(1)}, bf16[8,136,128]{2,1,0:T(8,128)(2,1)S(1)}, u32[]{:S(2)}, u32[]{:S(2)}) collective-permute-start(bf16[8,136,128]{2,1,0:T(8,128)(2,1)S(1)} %all-to-all-done.2.own_ref), channel_id=1, source_target_pairs={{0,1},{1,0},{2,3},{3,2},{4,5},{5,4},{6,7},{7,6},{8,9},{9,8},{10,11... | collective-permute-start | bytes 835592 | tf_op jit(solution)/shard_map/ppermute | solution.py:251
  56.4 3.1 %collective-permute-start.3 = (f32[16,1,16]{2,1,0:T(1,128)S(1)}, f32[16,1,16]{2,1,0:T(1,128)S(1)}, u32[]{:S(2)}, u32[]{:S(2)}) collective-permute-start(f32[16,1,16]{2,1,0:T(1,128)S(1)} %get-tuple-element.20), channel_id=1, source_target_pairs={{0,1},{1,0},{2,3},{3,2},{4,5},{5,4},{6,7},{7,6},{8,9},{9,8},{10,11... | collective-permute-start | bytes 3080 | tf_op jit(solution)/shard_map/ppermute | solution.py:259
  78.1 47.4 %all-to-all-start.4 = ((bf16[8,64,512]{2,1,0:T(8,128)(2,1)}), bf16[8,64,512]{2,1,0:T(8,128)(2,1)S(1)}, u32[]{:S(2)}, u32[]{:S(2)}) async-start(bf16[8,64,512]{2,1,0:T(8,128)(2,1)} %spread_share.1), calls=%async_computation.4 | async-start | bytes 1048576 | tf_op jit(solution)/shard_map/all_to_all | solution.py:37
  85.5 15.1 %collective-permute-start.6 = (bf16[2,2,256,128]{3,2,1,0:T(8,128)(2,1)S(1)}, bf16[2,2,256,128]{3,2,1,0:T(8,128)(2,1)S(1)}, u32[]{:S(2)}, u32[]{:S(2)}) collective-permute-start(bf16[2,2,256,128]{3,2,1,0:T(8,128)(2,1)S(1)} %get-tuple-element.24), channel_id=1, source_target_pairs={{0,96},{32,64},{64,32},{96,0},{1,97},{33,65},{65,33},{97,1},{2,98}... | collective-permute-start | bytes 786440 | tf_op jit(solution)/shard_map/ppermute | solution.py:255
  88.6 21.9 %collective-permute-start.5 = (bf16[2,2,256,128]{3,2,1,0:T(8,128)(2,1)S(1)}, bf16[2,2,256,128]{3,2,1,0:T(8,128)(2,1)S(1)}, u32[]{:S(2)}, u32[]{:S(2)}) collective-permute-start(bf16[2,2,256,128]{3,2,1,0:T(8,128)(2,1)S(1)} %get-tuple-element.23), channel_id=1, source_target_pairs={{0,64},{32,96},{64,0},{96,32},{1,65},{33,97},{65,1},{97,33},{2,66}... | collective-permute-start | bytes 786440 | tf_op jit(solution)/shard_map/ppermute | solution.py:255
  92.5 24.2 %collective-permute-start.4 = (bf16[2,2,256,128]{3,2,1,0:T(8,128)(2,1)S(1)}, bf16[2,2,256,128]{3,2,1,0:T(8,128)(2,1)S(1)}, u32[]{:S(2)}, u32[]{:S(2)}) collective-permute-start(bf16[2,2,256,128]{3,2,1,0:T(8,128)(2,1)S(1)} %get-tuple-element.22), channel_id=1, source_target_pairs={{0,32},{32,0},{64,96},{96,64},{1,33},{33,1},{65,97},{97,65},{2,34}... | collective-permute-start | bytes 786440 | tf_op jit(solution)/shard_map/ppermute | solution.py:255
  116.9 8.7 %collective-permute-start.7 = (bf16[4,2,256,128]{3,2,1,0:T(8,128)(2,1)S(1)}, bf16[4,2,256,128]{3,2,1,0:T(8,128)(2,1)S(1)}, u32[]{:S(2)}, u32[]{:S(2)}) collective-permute-start(bf16[4,2,256,128]{3,2,1,0:T(8,128)(2,1)S(1)} %pad_maximum_fusion), channel_id=1, source_target_pairs={{0,1},{1,0},{2,3},{3,2},{4,5},{5,4},{6,7},{7,6},{8,9},{9,8},{10,11... | collective-permute-start | bytes 1572872 | tf_op jit(solution)/shard_map/ppermute | solution.py:256
